TPU v7x, 32 devices: a 4x2x2 block of a 4x4x8 slice. The times are simulated.
32 devices in a mesh: dp: 4 (over y, z), dcp: 8 (over x, core).
Axes of the slice: x: 4, y: 2, z: 2, core: 2. Of those that a mesh axis runs over, the one named last changes fastest.
The devices are a block of a 4x4x8 slice.
Arguments:
- q_abs: bfloat16 [1024, 16, 576], P('dp', 'dcp'), parts along dimension 0
- latent_cache: bfloat16 [1024, 1, 8, 128, 576], P('dp', None, 'dcp'), parts along dimension 0
- ctx_len: int32 [1024], P('dp'), parts along dimension 0
Outputs:
- output: bfloat16 [1024, 16, 512], P(('dp', 'dcp')), parts along dimension 0
There are 4 independent parts. A program takes and returns all parts, laid end to end along the dimension named above; each array names one.
All inputs are finite; a program needn't handle non-finite values.
Results may differ from a plain program's by a relative error of at most 0.00763254.
Values are sent between devices in bfloat16 or wider.
A program may use at most 768 MiB of HBM per device.

v0:
```python
import jax
import jax.numpy as jnp
from jax import lax
from jax.sharding import PartitionSpec as P

ROPE_DIM = 64
QK_DIM = 192


def solution(mesh):
    group_size = mesh.shape['dcp']

    def local_step(q_blk, cache_blk, len_blk):
        batch_rows = q_blk.shape[0]
        num_pages = cache_blk.shape[1]
        page_len = cache_blk.shape[3]
        latent_dim = q_blk.shape[2] - ROPE_DIM
        out_rows = batch_rows // group_size
        dev_index = lax.axis_index('dcp')
        q_full = lax.all_gather(q_blk, 'dcp', axis=1, tiled=True)
        cache_own = cache_blk[:, :, 0]
        scores = jnp.einsum('bhw,bjtw->bhjt', q_full, cache_own, preferred_element_type=jnp.float32) * (QK_DIM ** -0.5)
        positions = (jnp.arange(num_pages)[:, None] * group_size + dev_index) * page_len + jnp.arange(page_len)[None, :]
        is_valid = positions[None] < len_blk[:, None, None]
        scores = jnp.where(is_valid[:, None], scores, -1e30)
        row_max = jnp.max(scores, axis=(2, 3))
        weights_exp = jnp.exp(scores - row_max[:, :, None, None])
        denom_sum = jnp.sum(weights_exp, axis=(2, 3))
        pv_sum = jnp.einsum('bhjt,bjtw->bhw', weights_exp.astype(jnp.bfloat16), cache_own, preferred_element_type=jnp.float32)
        part_out = (pv_sum[..., :latent_dim] / denom_sum[..., None]).astype(jnp.bfloat16)
        part_lse = row_max + jnp.log(denom_sum)
        recv_out = lax.all_to_all(part_out, 'dcp', 0, 0, tiled=True).reshape(group_size, out_rows, part_out.shape[1], latent_dim)
        recv_lse = lax.all_to_all(part_lse, 'dcp', 0, 0, tiled=True).reshape(group_size, out_rows, part_lse.shape[1])
        total_lse = jax.nn.logsumexp(recv_lse, axis=0)
        merge_weights = jnp.exp(recv_lse - total_lse[None])
        merged = jnp.sum(merge_weights[..., None] * recv_out.astype(jnp.float32), axis=0)
        return merged.astype(jnp.bfloat16)

    return jax.shard_map(local_step, mesh=mesh, in_specs=(P('dp', 'dcp', None), P('dp', None, 'dcp', None, None), P('dp')), out_specs=P(('dp', 'dcp'), None, None), check_vma=False)
```

profile of v0, /device:TPU:81, one launch (start us, length us, event | category | flops | bytes accessed | tf_op | source)
XLA Modules:
  0.0 156.0 jit_solution(1940094453225764697)
XLA Ops:
  6.5 0.0 all-gather.2.cloned.1.call-start
  6.6 0.7 all-gather.2.cloned.1.call-update
  7.3 0.8 broadcast_compare_fusion
  8.1 36.2 %all-gather.2.cloned.1.call-done = bf16[256,16,576]{0,2,1:T(8,128)(2,1)} async-done(((bf16[256,2,576]{0,2,1:T(8,128)(2,1)}), bf16[256,16,576]{0,2,1:T(8,128)(2,1)}) %all-gather.2.cloned.1.call-update) | async-done | bytes 4718608 | tf_op jit(solution)/shard_map/all_gather | solution.py:20
  44.3 8.9 %copy.16 = bf16[256,16,576]{2,1,0:T(8,128)(2,1)} copy(bf16[256,16,576]{0,2,1:T(8,128)(2,1)} %all-gather.2.cloned.1.call-done) | data formatting | bytes 9437184 | tf_op jit(solution)/shard_map/all_gather | solution.py:20
  53.3 16.2 %fusion.5 = (f32[256,16]{1,0:T(8,128)S(1)}, f32[256,16,128]{2,1,0:T(8,128)S(1)}) fusion(pred[256,128]{1,0:T(8,128)(4,1)S(1)} %broadcast_compare_fusion, bf16[256,16,576]{2,1,0:T(8,128)(2,1)} %copy.16, bf16[256,1,1,128,576]{3,4,2,1,0:T(8,128)(2,1)} %param.4), kind=kOutput, calls=%fused_computation.7 | convolution fusion | flops 605548544 | bytes 44613632 | tf_op jit(solution)/shard_map/bhw,bjtw->bhjt/dot_general | solution.py:22
  69.5 0.1 copy.18
  69.6 1.3 fusion.7
  70.9 0.1 copy.17
  70.9 0.1 add.32
  71.0 0.7 reshape.86
  71.7 3.5 %all-to-all-start = ((f32[8,1,512]{2,1,0:T(1,128)}), f32[8,1,512]{2,1,0:T(1,128)S(1)}, u32[]{:S(2)}, u32[]{:S(2)}) async-start(f32[8,1,512]{2,1,0:T(1,128)} %reshape.86), calls=%async_computation | async-start | bytes 32768 | tf_op jit(solution)/shard_map/all_to_all | solution.py:33
  75.3 16.8 %divide_convert_fusion = bf16[256,16,512]{2,1,0:T(8,128)(2,1)} fusion(f32[256,16]{1,0:T(8,128)S(1)} %fusion.7, bf16[256,128,576]{1,2,0:T(8,128)(2,1)} %bitcast.17, f32[256,16,128]{2,1,0:T(8,128)S(1)} %get-tuple-element.6, f32[256,16]{1,0:T(8,128)S(1)} %get-tuple-element.5, pred[256,128]{1,0:T(8,128)(4,1)S(1)} %broadcast_compare_fusion), kind=kOutput, calls=%fused_computation.4 | convolution fusion | flops 543162368 | bytes 39911424 | tf_op jit(solution)/shard_map/bhjt,bjtw->bhw/dot_general | solution.py:29
  92.0 0.0 all-to-all-done
  92.1 4.9 %all-to-all-start.1 = ((bf16[256,16,512]{2,1,0:T(8,128)(2,1)}), bf16[256,16,512]{2,1,0:T(8,128)(2,1)}, u32[]{:S(2)}, u32[]{:S(2)}) async-start(bf16[256,16,512]{2,1,0:T(8,128)(2,1)} %divide_convert_fusion), calls=%async_computation.1 | async-start | bytes 8388608 | tf_op jit(solution)/shard_map/all_to_all | solution.py:32
  96.9 0.5 broadcast.43
  97.4 0.7 reduce.4
  98.1 0.1 reshape.87
  98.3 0.1 copy.20
  98.4 47.1 %all-to-all-done.1 = bf16[256,16,512]{2,1,0:T(8,128)(2,1)} async-done(((bf16[256,16,512]{2,1,0:T(8,128)(2,1)}), bf16[256,16,512]{2,1,0:T(8,128)(2,1)}, u32[]{:S(2)}, u32[]{:S(2)}) %all-to-all-start.1) | async-done | bytes 4194336 | tf_op jit(solution)/shard_map/all_to_all | solution.py:32
  145.5 3.6 %fusion.2 = bf16[32,16,512]{2,1,0:T(8,128)(2,1)} fusion(bf16[8,32,16,512]{3,2,1,0:T(8,128)(2,1)} %bitcast.2, f32[8,32,16]{2,1,0:T(8,128)S(1)} %copy.20), kind=kLoop, calls=%fused_computation.3 | loop fusion | flops 6029312 | bytes 4734976 | tf_op jit(solution)/shard_map/reduce_sum | solution.py:36
  (8 shorter events, 0.1 us)
Async XLA Ops:
  6.5 37.8 %all-gather.2.cloned.1.call-start = ((), (), s32[]{:S(2)}) async-start(), calls=%async_computation.2 | async-start | bytes 5308416 | tf_op jit(solution)/shard_map/all_gather | solution.py:20
  71.7 20.3 %all-to-all-start = ((f32[8,1,512]{2,1,0:T(1,128)}), f32[8,1,512]{2,1,0:T(1,128)S(1)}, u32[]{:S(2)}, u32[]{:S(2)}) async-start(f32[8,1,512]{2,1,0:T(1,128)} %reshape.86), calls=%async_computation | async-start | bytes 32768 | tf_op jit(solution)/shard_map/all_to_all | solution.py:33
  92.1 53.4 %all-to-all-start.1 = ((bf16[256,16,512]{2,1,0:T(8,128)(2,1)}), bf16[256,16,512]{2,1,0:T(8,128)(2,1)}, u32[]{:S(2)}, u32[]{:S(2)}) async-start(bf16[256,16,512]{2,1,0:T(8,128)(2,1)} %divide_convert_fusion), calls=%async_computation.1 | async-start | bytes 8388608 | tf_op jit(solution)/shard_map/all_to_all | solution.py:32
Sparse Core Ops, SparseCore 0:
  8.9 35.3 all-gather.1
where the time goes:
time: 156 us
  waiting for transfers between devices  84.1 us (54%)
  matrix products  33 us (21%)
  between operations  13.5 us (9%)
  local copies, waits for them, and re-layouts  10.5 us (7%)
  starting transfers between devices  8.4 us (5%)
  other arithmetic  6.49 us (4%)
    all_to_all x1, waiting for transfers between devices, local_step(): lax.all_to_all(part_out, 'dcp', 0, 0, tiled=True)  47.1 us
    all_gather x1, waiting for transfers between devices, local_step(): q_full = lax.all_gather(q_blk, 'dcp', axis=1, tiled=True)  36.2 us
    dot_general x1, matrix products, local_step(): jnp.einsum('bhjt,bjtw->bhw', weights_exp.astype(jnp.bfloat16), cache_own,...  16.8 us
    dot_general x1, matrix products, local_step(): jnp.einsum('bhw,bjtw->bhjt', q_full, cache_own, preferred_element_type=jn...  16.2 us
    all_gather x1, local copies, waits for them, and re-layouts, local_step(): q_full = lax.all_gather(q_blk, 'dcp', axis=1, tiled=True)  8.93 us
    all_to_all x1, starting transfers between devices, local_step(): lax.all_to_all(part_out, 'dcp', 0, 0, tiled=True)  4.88 us
    reduce_sum x1, other arithmetic, local_step(): jnp.sum(merge_weights[..., None] * recv_out.astype(jnp.float32), axis=0)  3.64 us
    all_to_all x1, starting transfers between devices, local_step(): lax.all_to_all(part_lse, 'dcp', 0, 0, tiled=True)  3.52 us
  transfers between devices with their start and end apart: 3, of which 2 were waited for; matrix products, arithmetic and copies ran while one was open for 12% of the time, Pallas kernels for 0%

commit v1 on v0

v1 whole, which is shorter than its diff:
```python
import functools

import jax
import jax.numpy as jnp
from jax import lax
from jax.experimental import pallas as pl
from jax.experimental.pallas import tpu as pltpu
from jax.sharding import PartitionSpec as P

ROPE_DIM = 64
QK_DIM = 192
CORES = 2
STEP = 4
LANES = 128
MESH = pl.DeviceIdType.MESH
F32, BF16 = jnp.float32, jnp.bfloat16


def kernel(group, q_ref, cache_ref, len_ref, out_ref,
           qr, cv, q32, ob, ol, ri, rl, rf, rfl, ff, fl, fb, fbl, fp, fpl,
           q_in, c_in, q_send, q_recv, o_send, r_recv, f_recv, b_recv, p_recv):
    chips = group // CORES
    batch, width, page = cv.shape
    latent = width - ROPE_DIM
    heads = 2 * group
    blk = batch // chips
    core_rows = batch // group
    unit = core_rows // 2
    scale = QK_DIM ** -0.5
    tiles = [(lo, min(lo + LANES, width)) for lo in range(0, width, LANES)]

    me = lax.axis_index('dcp')
    x, k = me // CORES, me % CORES
    xr, xl, xf = (x + 1) % chips, (x + chips - 1) % chips, (x + 2) % chips
    other = 1 - k
    right, left, far, partner = xr * CORES + k, xl * CORES + k, xf * CORES + k, x * CORES + other

    def remote(src, dst, send, recv, dev):
        return pltpu.make_async_remote_copy(src_ref=src, dst_ref=dst, send_sem=send, recv_sem=recv,
                                            device_id={'dcp': dev}, device_id_type=MESH)

    order = [(2, 0, 0), (2, 0, 1), (2, 1, 0), (2, 1, 1),
             (-1, 'o', 0), (1, 'o', 1), (-1, 's', 0), (1, 's', 1),
             (-1, 0, 1), (1, 0, 0), (-1, 1, 1), (1, 1, 0),
             (0, 'o', 0), (0, 'o', 1), (0, 's', 0), (0, 's', 1)]

    def core_of(c):
        return other if c == 'o' else k if c == 's' else c

    def first_row(u):
        r, c, half = order[u]
        return pl.multiple_of((((x + r + chips) % chips) * CORES + core_of(c)) * core_rows + half * unit, unit)

    def cache_copy(u):
        rows = pl.ds(first_row(u), unit)
        return pltpu.make_async_copy(cache_ref.at[rows], cv.at[rows], c_in.at[u])

    own_q = pltpu.make_async_copy(q_ref, qr.at[me], q_in)
    own_q.start()
    for u in range(len(order)):
        cache_copy(u).start()

    barrier = pltpu.get_barrier_semaphore()
    peers = [partner] + [c * CORES + i for c in (xl, xr) for i in range(CORES)]
    for dev in peers:
        pl.semaphore_signal(barrier, inc=1, device_id={'dcp': dev}, device_id_type=MESH)
    pl.semaphore_wait(barrier, len(peers))
    own_q.wait()

    sends = []

    def q_copy(src, y, s, dev, n):
        rows = pl.ds(pl.multiple_of(((y + s) % chips) * blk, blk), blk)
        part = qr.at[src, :, rows, :]
        return remote(part, part, q_send.at[n], q_recv.at[src, s], dev)

    def q_start(src, y, s, dev):
        c = q_copy(src, y, s, dev, len(sends))
        c.start()
        sends.append(c)

    def q_wait(src, y, s):
        q_copy(src, y, s, partner, 0).wait_recv()

    to_right, to_left = [3, 0, 1, 2], [1, 2, 3, 0]
    for i in range(chips):
        q_start(me, x, to_right[i], right)
        q_start(me, x, to_left[i], left)
    for i in range(chips):
        q_start(me, x, i, partner)
    for i in range(chips):
        s = to_right[i]
        q_wait(left, xl, s)
        if s in (0, 1):
            q_start(left, xl, s, right)
        q_start(left, xl, s, partner)
        s = to_left[i]
        q_wait(right, xr, s)
        if s in (2, 3):
            q_start(right, xr, s, left)
        q_start(right, xr, s, partner)
    for s in (0, 2, 1, 3):
        q_wait(far, xf, s)
        q_start(far, xf, s, partner)
    for y in (x, xl, xr, xf):
        for s in range(chips):
            q_wait(y * CORES + other, y, s)

    lane = lax.broadcasted_iota(jnp.int32, (heads, page), 1)
    position = lane + me * page

    def compute(u):
        row0 = first_row(u)
        cache_copy(u).wait()
        for h in range(heads):
            for t, (lo, hi) in enumerate(tiles):
                q32[t, pl.ds(h * unit, unit), pl.ds(0, hi - lo)] = qr[h // 2, h % 2, pl.ds(row0, unit), pl.ds(lo, hi - lo)].astype(F32)

        def body(i, lse):
            for j in range(STEP):
                b = i * STEP + j
                q_b = jnp.concatenate([q32[t, pl.ds(b, heads, stride=unit), :][:, :hi - lo].astype(BF16)
                                       for t, (lo, hi) in enumerate(tiles)], axis=1)
                c_b = cv[row0 + b]
                s = jnp.dot(q_b, c_b, preferred_element_type=F32) * scale
                s = jnp.where(position < len_ref[row0 + b], s, -1e30)
                m = jnp.max(s, axis=1, keepdims=True)
                w = jnp.exp(s - m)
                l = jnp.sum(w, axis=1, keepdims=True)
                o = lax.dot_general(w.astype(BF16), c_b[:latent], (((1,), (1,)), ((), ())),
                                    preferred_element_type=F32)
                ob[u, b] = (o * (1.0 / l)).astype(BF16)
                lse = jnp.where(lane == b, m + jnp.log(l), lse)
            return lse

        ol[u] = lax.fori_loop(0, unit // STEP, body, jnp.zeros((heads, page), F32))

    def combine(terms, store):
        ls = [l[...] for _, l in terms]
        m = functools.reduce(jnp.maximum, ls)
        es = [jnp.exp(l - m) for l in ls]
        total = functools.reduce(jnp.add, es)
        ws = [e * (1.0 / total) for e in es]

        def body(i, carry):
            for j in range(STEP):
                b = i * STEP + j
                acc = None
                for (o, _), w in zip(terms, ws):
                    w_b = jnp.sum(jnp.where(lane == b, w, 0.0), axis=1, keepdims=True)
                    t = w_b * o[b].astype(F32)
                    acc = t if acc is None else acc + t
                store(b, acc)
            return carry

        lax.fori_loop(0, unit // STEP, body, 0)
        return m + jnp.log(total)

    n_out = [0]

    def send(o, l, o_dst, l_dst, sem, dev):
        for src, dst, s in ((o, o_dst, sem.at[0]), (l, l_dst, sem.at[1])):
            c = remote(src, dst, o_send.at[n_out[0]], s, dev)
            c.start()
            n_out[0] += 1
            sends.append(c)

    def arrived(o_dst, l_dst, sem):
        for dst, s in ((o_dst, sem.at[0]), (l_dst, sem.at[1])):
            remote(dst, dst, o_send.at[0], s, partner).wait_recv()

    def relay(way):
        for i in range(3):
            arrived(ri.at[way, i], rl.at[way, i], r_recv.at[way, i])
        mine = order.index((-1, 's', 0) if way == 0 else (1, 's', 1))
        terms = [(ob.at[mine], ol.at[mine])] + [(ri.at[way, i], rl.at[way, i]) for i in range(3)]

        def store(b, acc):
            rf[way, b] = acc

        rfl[way] = combine(terms, store)
        send(rf.at[way], rfl.at[way], ff.at[way], fl.at[way], f_recv.at[way], left if way == 0 else right)

    for u, (r, c, half) in enumerate(order):
        compute(u)
        o, l = ob.at[u], ol.at[u]
        if r == 2:
            dev = (xl if half == 0 else xr) * CORES + c
            send(o, l, ri.at[half, k], rl.at[half, k], r_recv.at[half, k], dev)
        elif r == 0:
            if c == 'o':
                send(o, l, fp.at[half], fpl.at[half], p_recv.at[half], partner)
        elif (r == -1) == (half == 0):
            if c == 'o':
                send(o, l, ri.at[half, 2], rl.at[half, 2], r_recv.at[half, 2], partner)
        else:
            dev = (xl if r == -1 else xr) * CORES + c
            send(o, l, fb.at[half, k], fbl.at[half, k], b_recv.at[half, k], dev)
        if u == 9:
            relay(0)
            relay(1)

    for half in range(2):
        arrived(fp.at[half], fpl.at[half], p_recv.at[half])
        for i in range(CORES):
            arrived(fb.at[half, i], fbl.at[half, i], b_recv.at[half, i])
        arrived(ff.at[half], fl.at[half], f_recv.at[half])
        mine = order.index((0, 's', half))
        terms = [(ob.at[mine], ol.at[mine]), (fp.at[half], fpl.at[half])]
        terms += [(fb.at[half, i], fbl.at[half, i]) for i in range(CORES)]
        terms += [(ff.at[half], fl.at[half])]

        def store(b, acc):
            out_ref[half * unit + b] = acc.astype(BF16)

        combine(terms, store)

    for c in sends:
        c.wait_send()


def solution(mesh):
    group = mesh.shape['dcp']
    chips = group // CORES

    def local_step(q_blk, cache_blk, len_blk):
        batch, _, width = q_blk.shape
        page = cache_blk.shape[3]
        latent = width - ROPE_DIM
        heads = 2 * group
        rows = batch // group
        unit = rows // 2
        units = batch // unit
        q_own = jnp.transpose(q_blk, (1, 0, 2))
        cache_own = jnp.transpose(cache_blk[:, 0, 0], (0, 2, 1))
        any_spec = pl.BlockSpec(memory_space=pl.ANY)
        dma = pltpu.SemaphoreType.DMA
        return pl.pallas_call(
            functools.partial(kernel, group),
            out_shape=jax.ShapeDtypeStruct((rows, heads, latent), BF16),
            in_specs=[any_spec, any_spec, pl.BlockSpec(memory_space=pltpu.SMEM)],
            out_specs=pl.BlockSpec(memory_space=pltpu.VMEM),
            scratch_shapes=[
                pltpu.VMEM((group, 2, batch, width), BF16),
                pltpu.VMEM((batch, width, page), BF16),
                pltpu.VMEM((pl.cdiv(width, LANES), heads * unit, LANES), F32),
                pltpu.VMEM((units, unit, heads, latent), BF16),
                pltpu.VMEM((units, heads, page), F32),
                pltpu.VMEM((2, 3, unit, heads, latent), BF16),
                pltpu.VMEM((2, 3, heads, page), F32),
                pltpu.VMEM((2, unit, heads, latent), F32),
                pltpu.VMEM((2, heads, page), F32),
                pltpu.VMEM((2, unit, heads, latent), F32),
                pltpu.VMEM((2, heads, page), F32),
                pltpu.VMEM((2, CORES, unit, heads, latent), BF16),
                pltpu.VMEM((2, CORES, heads, page), F32),
                pltpu.VMEM((2, unit, heads, latent), BF16),
                pltpu.VMEM((2, heads, page), F32),
                dma(()),
                dma((units,)),
                dma((28,)),
                dma((group, chips)),
                dma((32,)),
                dma((2, 3, 2)),
                dma((2, 2)),
                dma((2, CORES, 2)),
                dma((2, 2)),
            ],
            compiler_params=pltpu.CompilerParams(collective_id=0, has_side_effects=True,
                                                 vmem_limit_bytes=67043328),
        )(q_own, cache_own, len_blk)

    return jax.shard_map(local_step, mesh=mesh, in_specs=(P('dp', 'dcp', None), P('dp', None, 'dcp', None, None), P('dp')), out_specs=P(('dp', 'dcp'), None, None), check_vma=False)
```

time: 156 us -> 113 us (0.72)
  Pallas kernels: 0 us -> 109 us
  waiting for transfers between devices: 84.1 us -> 0 us
  matrix products: 33 us -> 0 us
  between operations: 13.5 us -> 0.01 us
  starting transfers between devices: 8.4 us -> 0 us
  other arithmetic: 6.49 us -> 0 us
  local copies, waits for them, and re-layouts: 10.5 us -> 4.01 us
    pallas_call x0 -> x1, Pallas kernels: none -> 109 us  [local_step(): pl.pallas_call(functools.partial(kernel, group), out_shape=jax.ShapeDtype...]
    all_to_all x2 -> x0, waiting for transfers between devices: 47.1 us -> none  [the longest x1 47.1 us: local_step(): lax.all_to_all(part_out, 'dcp', 0, 0, tiled=True)]
    all_gather x1 -> x0, waiting for transfers between devices: 36.2 us -> none  [local_step(): q_full = lax.all_gather(q_blk, 'dcp', axis=1, tiled=True)]
    dot_general x2 -> x0, matrix products: 33 us -> none  [the longest x1 16.8 us: local_step(): jnp.einsum('bhjt,bjtw->bhw', weights_exp.astype(jnp.bfloat16), cache_own,...]
    all_gather x1 -> x0, local copies, waits for them, and re-layouts: 8.93 us -> none  [local_step(): q_full = lax.all_gather(q_blk, 'dcp', axis=1, tiled=True)]
    all_to_all x2 -> x0, starting transfers between devices: 8.4 us -> none  [the longest x1 4.88 us: local_step(): lax.all_to_all(part_out, 'dcp', 0, 0, tiled=True)]
    reduce_sum x3 -> x0, other arithmetic: 4.96 us -> none  [the longest x1 3.64 us: local_step(): jnp.sum(merge_weights[..., None] * recv_out.astype(jnp.float32), axis=0)]
    unnamed x2, local copies, waits for them, and re-layouts: 0.78 us -> 4.01 us
  transfers between devices with their start and end apart: 3 -> 0, of which waited for: 2 -> 0; matrix products, arithmetic and copies ran while one was open for 12% -> 0% of each run, Pallas kernels for 0% -> 0%
where the time goes in v1:
time: 113 us
  Pallas kernels  109 us (96%)
  local copies, waits for them, and re-layouts  4.01 us (4%)
    pallas_call x1, Pallas kernels, local_step(): pl.pallas_call(functools.partial(kernel, group), out_shape=jax.ShapeDtype...  109 us
    unnamed x2, local copies, waits for them, and re-layouts  4.01 us

profile of v1, /device:TPU:81, one launch (start us, length us, event | category | flops | bytes accessed | tf_op | source)
XLA Modules:
  0.0 112.9 jit_solution(7373417996588833087)
XLA Ops:
  0.0 2.1 %copy.4 = bf16[256,2,576]{2,0,1:T(8,128)(2,1)} copy(bf16[256,2,576]{0,2,1:T(8,128)(2,1)} %param.3) | data formatting | bytes 1179648 | tf_op args[0]
  2.1 108.9 %shard_map.37 = bf16[32,16,512]{2,1,0:T(8,128)(2,1)} custom-call(bf16[2,256,576]{2,1,0:T(8,128)(2,1)} %bitcast.5, bf16[256,576,128]{2,1,0:T(8,128)(2,1)} %bitcast.4, s32[256]{0:T(256)} %len_ref.1), custom_call_target="tpu_custom_call" | custom-call | tf_op jit(solution)/shard_map/pallas_call | solution.py:238
  111.0 1.9 %copy.6 = bf16[32,16,512]{2,1,0:T(8,128)(2,1)} copy(bf16[32,16,512]{2,1,0:T(8,128)(2,1)} %shard_map.37) | data formatting | bytes 1048576

commit v2 on v1

--- a/solution.py
+++ b/solution.py
@@ -10,14 +10,15 @@
 ROPE_DIM = 64
 QK_DIM = 192
 CORES = 2
-STEP = 4
+STEP = 16
+MERGE_STEP = 4
 LANES = 128
 MESH = pl.DeviceIdType.MESH
 F32, BF16 = jnp.float32, jnp.bfloat16
 
 
 def kernel(group, q_ref, cache_ref, len_ref, out_ref,
-           qr, cv, q32, ob, ol, ri, rl, rf, rfl, ff, fl, fb, fbl, fp, fpl,
+           qr, cv, q32, sb, wb, ib, ob, ol, ri, rl, rf, rfl, ff, fl, fb, fbl, fp, fpl,
            q_in, c_in, q_send, q_recv, o_send, r_recv, f_recv, b_recv, p_recv):
     chips = group // CORES
     batch, width, page = cv.shape
@@ -26,6 +27,7 @@
     blk = batch // chips
     core_rows = batch // group
     unit = core_rows // 2
+    units = batch // unit
     scale = QK_DIM ** -0.5
     tiles = [(lo, min(lo + LANES, width)) for lo in range(0, width, LANES)]
 
@@ -57,9 +59,6 @@
 
     own_q = pltpu.make_async_copy(q_ref, qr.at[me], q_in)
     own_q.start()
-    for u in range(len(order)):
-        cache_copy(u).start()
-
     barrier = pltpu.get_barrier_semaphore()
     peers = [partner] + [c * CORES + i for c in (xl, xr) for i in range(CORES)]
     for dev in peers:
@@ -88,6 +87,8 @@
         q_start(me, x, to_left[i], left)
     for i in range(chips):
         q_start(me, x, i, partner)
+    for u in range(units):
+        cache_copy(u).start()
     for i in range(chips):
         s = to_right[i]
         q_wait(left, xl, s)
@@ -109,31 +110,45 @@
     lane = lax.broadcasted_iota(jnp.int32, (heads, page), 1)
     position = lane + me * page
 
-    def compute(u):
-        row0 = first_row(u)
-        cache_copy(u).wait()
-        for h in range(heads):
-            for t, (lo, hi) in enumerate(tiles):
-                q32[t, pl.ds(h * unit, unit), pl.ds(0, hi - lo)] = qr[h // 2, h % 2, pl.ds(row0, unit), pl.ds(lo, hi - lo)].astype(F32)
+    def stage(t):
+        u_qk, u_sm, u_pv = t if t < units else None, t - 1 if 1 <= t <= units else None, t - 2 if t >= 2 else None
+        if u_qk is not None:
+            row0 = first_row(u_qk)
+            cache_copy(u_qk).wait()
+            for h in range(heads):
+                for c, (lo, hi) in enumerate(tiles):
+                    q32[c, pl.ds(h * unit, unit), pl.ds(0, hi - lo)] = qr[h // 2, h % 2, pl.ds(row0, unit), pl.ds(lo, hi - lo)].astype(F32)
+        if u_sm is not None:
+            sm_row0 = first_row(u_sm)
+        if u_pv is not None:
+            pv_row0 = first_row(u_pv)
 
         def body(i, lse):
             for j in range(STEP):
                 b = i * STEP + j
-                q_b = jnp.concatenate([q32[t, pl.ds(b, heads, stride=unit), :][:, :hi - lo].astype(BF16)
-                                       for t, (lo, hi) in enumerate(tiles)], axis=1)
-                c_b = cv[row0 + b]
-                s = jnp.dot(q_b, c_b, preferred_element_type=F32) * scale
-                s = jnp.where(position < len_ref[row0 + b], s, -1e30)
-                m = jnp.max(s, axis=1, keepdims=True)
-                w = jnp.exp(s - m)
-                l = jnp.sum(w, axis=1, keepdims=True)
-                o = lax.dot_general(w.astype(BF16), c_b[:latent], (((1,), (1,)), ((), ())),
-                                    preferred_element_type=F32)
-                ob[u, b] = (o * (1.0 / l)).astype(BF16)
-                lse = jnp.where(lane == b, m + jnp.log(l), lse)
+                if u_sm is not None:
+                    s = sb[u_sm % 2, b] * scale
+                    s = jnp.where(position < len_ref[sm_row0 + b], s, -1e30)
+                    m = jnp.max(s, axis=1, keepdims=True)
+                    w = jnp.exp(s - m)
+                    l = jnp.sum(w, axis=1, keepdims=True)
+                    lse = jnp.where(lane == b, m + jnp.log(l), lse)
+                if u_qk is not None:
+                    q_b = jnp.concatenate([q32[c, pl.ds(b, heads, stride=unit), :][:, :hi - lo].astype(BF16)
+                                           for c, (lo, hi) in enumerate(tiles)], axis=1)
+                    sb[u_qk % 2, b] = jnp.dot(q_b, cv[row0 + b], preferred_element_type=F32)
+                if u_pv is not None:
+                    o = lax.dot_general(wb[u_pv % 2, b], cv[pv_row0 + b, :latent, :], (((1,), (1,)), ((), ())),
+                                        preferred_element_type=F32)
+                    ob[u_pv, b] = (o * jnp.concatenate([ib[u_pv % 2, b]] * (latent // page), axis=1)).astype(BF16)
+                if u_sm is not None:
+                    wb[u_sm % 2, b] = w.astype(BF16)
+                    ib[u_sm % 2, b] = jnp.broadcast_to(1.0 / l, (heads, page))
             return lse
 
-        ol[u] = lax.fori_loop(0, unit // STEP, body, jnp.zeros((heads, page), F32))
+        lse = lax.fori_loop(0, unit // STEP, body, jnp.zeros((heads, page), F32))
+        if u_sm is not None:
+            ol[u_sm] = lse
 
     def combine(terms, store):
         ls = [l[...] for _, l in terms]
@@ -143,8 +158,8 @@
         ws = [e * (1.0 / total) for e in es]
 
         def body(i, carry):
-            for j in range(STEP):
-                b = i * STEP + j
+            for j in range(MERGE_STEP):
+                b = i * MERGE_STEP + j
                 acc = None
                 for (o, _), w in zip(terms, ws):
                     w_b = jnp.sum(jnp.where(lane == b, w, 0.0), axis=1, keepdims=True)
@@ -153,7 +168,7 @@
                 store(b, acc)
             return carry
 
-        lax.fori_loop(0, unit // STEP, body, 0)
+        lax.fori_loop(0, unit // MERGE_STEP, body, 0)
         return m + jnp.log(total)
 
     n_out = [0]
@@ -181,8 +196,12 @@
         rfl[way] = combine(terms, store)
         send(rf.at[way], rfl.at[way], ff.at[way], fl.at[way], f_recv.at[way], left if way == 0 else right)
 
-    for u, (r, c, half) in enumerate(order):
-        compute(u)
+    for t in range(units + 2):
+        stage(t)
+        if t < 2:
+            continue
+        u = t - 2
+        r, c, half = order[u]
         o, l = ob.at[u], ol.at[u]
         if r == 2:
             dev = (xl if half == 0 else xr) * CORES + c
@@ -244,6 +263,9 @@
                 pltpu.VMEM((group, 2, batch, width), BF16),
                 pltpu.VMEM((batch, width, page), BF16),
                 pltpu.VMEM((pl.cdiv(width, LANES), heads * unit, LANES), F32),
+                pltpu.VMEM((2, unit, heads, page), F32),
+                pltpu.VMEM((2, unit, heads, page), BF16),
+                pltpu.VMEM((2, unit, heads, page), F32),
                 pltpu.VMEM((units, unit, heads, latent), BF16),
                 pltpu.VMEM((units, heads, page), F32),
                 pltpu.VMEM((2, 3, unit, heads, latent), BF16),

time: 113 us -> 77.4 us (0.68)
  Pallas kernels: 109 us -> 73.1 us
    pallas_call x1, Pallas kernels: 109 us -> 73.1 us  [local_step(): pl.pallas_call(functools.partial(kernel, group), out_shape=jax.ShapeDtype...]
where the time goes in v2:
time: 77.4 us; the launch traced here: 77.1 us
  Pallas kernels  73.1 us (94%)
  local copies, waits for them, and re-layouts  4.01 us (5%)
    pallas_call x1, Pallas kernels, local_step(): pl.pallas_call(functools.partial(kernel, group), out_shape=jax.ShapeDtype...  73.1 us
    unnamed x2, local copies, waits for them, and re-layouts  4.01 us

profile of v2, /device:TPU:81, one launch (start us, length us, event | category | flops | bytes accessed | tf_op | source)
XLA Modules:
  0.0 77.1 jit_solution(3824384910795140361)
XLA Ops:
  0.0 2.1 %copy.4 = bf16[256,2,576]{2,0,1:T(8,128)(2,1)} copy(bf16[256,2,576]{0,2,1:T(8,128)(2,1)} %param.3) | data formatting | bytes 1179648 | tf_op args[0]
  2.1 73.1 %shard_map.37 = bf16[32,16,512]{2,1,0:T(8,128)(2,1)} custom-call(bf16[2,256,576]{2,1,0:T(8,128)(2,1)} %bitcast.5, bf16[256,576,128]{2,1,0:T(8,128)(2,1)} %bitcast.4, s32[256]{0:T(256)} %len_ref.1), custom_call_target="tpu_custom_call" | custom-call | tf_op jit(solution)/shard_map/pallas_call | solution.py:257
  75.3 1.9 %copy.6 = bf16[32,16,512]{2,1,0:T(8,128)(2,1)} copy(bf16[32,16,512]{2,1,0:T(8,128)(2,1)} %shard_map.37) | data formatting | bytes 1048576

commit v3 on v2

v3 whole, which is shorter than its diff:
```python
import functools

import jax
import jax.numpy as jnp
from jax import lax
from jax.experimental import pallas as pl
from jax.experimental.pallas import tpu as pltpu
from jax.sharding import PartitionSpec as P

ROPE_DIM = 64
QK_DIM = 192
CORES = 2
LANES = 128
STEP = 8
MERGE_STEP = 4
PIECES = 2
MESH = pl.DeviceIdType.MESH
F32, BF16 = jnp.float32, jnp.bfloat16

ORDER = [(2, 0, 0), (2, 0, 1), (2, 1, 0), (2, 1, 1),
         (1, 'o', 1), (1, 0, 0), (1, 1, 0), (1, 's', 1),
         (-1, 'o', 0), (-1, 0, 1), (-1, 1, 1), (-1, 's', 0),
         (0, 'o', 0), (0, 'o', 1), (0, 's', 0), (0, 's', 1)]
RELAY_AFTER = 15


def kernel(group, q_ref, cache_ref, len_ref, res,
           qraw, qb0, qb1, qb2, qb3, cv, q32, sb, wb, ib, ob, ol, ri, rl, rf, rfl, ff, fl, fb, fbl, fp, fpl, lo, lol,
           q_in, c_in, q_send, q_recv, o_send, r_recv, f_recv, b_recv, p_recv):
    chips = group // CORES
    batch, width, page = cv.shape
    latent = width - ROPE_DIM
    heads = 2 * group
    blk = batch // chips
    core_rows = batch // group
    unit = core_rows // 2
    units = batch // unit
    piece = unit // PIECES
    scale = QK_DIM ** -0.5

    me = lax.axis_index('dcp')
    x, k = me // CORES, me % CORES
    xr, xl, xf = (x + 1) % chips, (x + chips - 1) % chips, (x + 2) % chips
    other = 1 - k
    right, left, far, partner = xr * CORES + k, xl * CORES + k, xf * CORES + k, x * CORES + other

    def remote(src, dst, send, recv, dev):
        return pltpu.make_async_remote_copy(src_ref=src, dst_ref=dst, send_sem=send, recv_sem=recv,
                                            device_id={'dcp': dev}, device_id_type=MESH)

    def core_of(c):
        return other if c == 'o' else k if c == 's' else c

    def first_row(u):
        r, c, half = ORDER[u]
        return pl.multiple_of((((x + r + chips) % chips) * CORES + core_of(c)) * core_rows + half * unit, unit)

    def cache_copy(u):
        rows = pl.ds(first_row(u), unit)
        return pltpu.make_async_copy(cache_ref.at[rows], cv.at[rows], c_in.at[u])

    blocks = [qb0, qb1, qb2, qb3]
    own_q = pltpu.make_async_copy(q_ref, qraw, q_in)
    own_q.start()

    barrier = pltpu.get_barrier_semaphore()
    peers = [partner] + [c * CORES + i for c in (xl, xr) for i in range(CORES)]
    for dev in peers:
        pl.semaphore_signal(barrier, inc=1, device_id={'dcp': dev}, device_id_type=MESH)

    own_q.wait()
    for s in range(chips):
        first = ((x + s) % chips) * blk
        cols = pl.ds(pl.multiple_of(first // LANES * LANES, LANES), LANES)
        pick = jnp.where(lax.broadcasted_iota(jnp.int32, (blk, LANES), 1) == lax.broadcasted_iota(jnp.int32, (blk, LANES), 0) + first % LANES, 1.0, 0.0).astype(BF16)
        parts = [qraw[h, c * LANES:(c + 1) * LANES, cols] for h in range(2) for c in range(latent // LANES)]
        parts.append(jnp.concatenate([qraw[h, latent:, cols] for h in range(2)], axis=0))
        for c, part in enumerate(parts):
            rows = lax.dot_general(pick, part, (((1,), (1,)), ((), ())), preferred_element_type=F32)
            blocks[s][me, :, c * LANES:(c + 1) * LANES] = rows.astype(BF16)
    pl.semaphore_wait(barrier, len(peers))

    sends = []
    ME, RIGHT, FAR, LEFT = 0, 1, 2, 3

    def q_copy(src, y, s, dev, to, n):
        return remote(blocks[(y + s) % chips].at[src], blocks[(y + s - to) % chips].at[src], q_send.at[n], q_recv.at[src, s], dev)

    def q_start(src, y, s, dev, to):
        c = q_copy(src, y, s, dev, to, len(sends))
        c.start()
        sends.append(c)

    def q_wait(src, y, s):
        q_copy(src, y, s, partner, 0, 0).wait_recv()

    def go(s, to):
        q_start(me, 0, s, {ME: partner, RIGHT: right, LEFT: left}[to], to)

    def take(y, s, then=None):
        src = {RIGHT: right, FAR: far, LEFT: left}[y]
        q_wait(src, y, s)
        if then is not None:
            q_start(src, y, s, {RIGHT: right, LEFT: left}[then], then)
        q_start(src, y, s, partner, 0)

    def from_partner(own, from_left, from_right, from_far):
        for y, c, s in ((ME, x, own), (LEFT, xl, from_left), (RIGHT, xr, from_right), (FAR, xf, from_far)):
            q_wait(c * CORES + other, y, s)

    go(0, RIGHT)
    go(1, LEFT)
    go(3, RIGHT)
    go(3, LEFT)
    go(2, ME)
    go(2, LEFT)
    for u in range(units):
        cache_copy(u).start()
    for s in (1, 3, 0):
        go(s, ME)
    take(LEFT, 0, RIGHT)
    go(1, RIGHT)
    take(RIGHT, 1)
    take(LEFT, 3)
    go(2, RIGHT)
    take(RIGHT, 3, LEFT)
    go(0, LEFT)
    take(FAR, 0)
    take(RIGHT, 2, LEFT)
    from_partner(2, 3, 1, 0)

    def slot4():
        take(LEFT, 1, RIGHT)
        take(FAR, 3)

    def slot5():
        take(LEFT, 2)
        take(RIGHT, 0)
        from_partner(1, 2, 0, 3)

    def slot6():
        take(FAR, 1)
        take(FAR, 2)
        from_partner(3, 0, 2, 1)
        from_partner(0, 1, 3, 2)

    before = {}
    slot4()
    slot5()
    slot6()

    lane = lax.broadcasted_iota(jnp.int32, (heads, page), 1)
    position = lane + me * page
    rope_lane = lax.broadcasted_iota(jnp.int32, (unit, LANES), 1)
    of_head = [rope_lane < ROPE_DIM, rope_lane >= ROPE_DIM]

    def stage(t):
        u_qk, u_sm, u_pv = t if t < units else None, t - 1 if 1 <= t <= units else None, t - 2 if t >= 2 else None
        if u_qk is not None:
            row0 = first_row(u_qk)
            cache_copy(u_qk).wait()
            r, c, half = ORDER[u_qk]
            q_block = blocks[r % chips]
            q_rows = pl.ds(pl.multiple_of(core_of(c) * core_rows + half * unit, unit), unit)

            def fill(d, carry):
                for h in range(2):
                    rows = pl.ds(pl.multiple_of((d * 2 + h) * unit, unit), unit)
                    for c in range(latent // LANES):
                        q32[c, rows, :] = q_block[d, q_rows, pl.ds(h * latent + c * LANES, LANES)].astype(F32)
                    rope = q_block[d, q_rows, pl.ds(2 * latent, LANES)].astype(F32)
                    q32[latent // LANES, rows, :] = jnp.where(of_head[h], rope, 0.0)
                return carry

            lax.fori_loop(0, group, fill, 0)
        if u_sm is not None:
            sm_row0 = first_row(u_sm)
        if u_pv is not None:
            pv_row0 = first_row(u_pv)

        def body(i, lse):
            for j in range(STEP):
                b = i * STEP + j
                if u_sm is not None:
                    s = sb[u_sm % 2, b] * scale
                    s = jnp.where(position < len_ref[sm_row0 + b], s, -1e30)
                    m = jnp.max(s, axis=1, keepdims=True)
                    w = jnp.exp(s - m)
                    l = jnp.sum(w, axis=1, keepdims=True)
                    lse = jnp.where(lane == b, m + jnp.log(l), lse)
                if u_qk is not None:
                    q_b = jnp.concatenate([q32[c, pl.ds(b, heads, stride=unit), :].astype(BF16)
                                           for c in range(latent // LANES + 1)], axis=1)
                    c_b = jnp.concatenate([cv[row0 + b], cv[row0 + b, latent:, :]], axis=0)
                    sb[u_qk % 2, b] = jnp.dot(q_b, c_b, preferred_element_type=F32)
                if u_pv is not None:
                    o = lax.dot_general(wb[u_pv % 2, b], cv[pv_row0 + b, :latent, :], (((1,), (1,)), ((), ())),
                                        preferred_element_type=F32)
                    ob[u_pv, b] = (o * jnp.concatenate([ib[u_pv % 2, b]] * (latent // page), axis=1)).astype(BF16)
                if u_sm is not None:
                    wb[u_sm % 2, b] = w.astype(BF16)
                    ib[u_sm % 2, b] = jnp.broadcast_to(1.0 / l, (heads, page))
            return lse

        lse = lax.fori_loop(0, unit // STEP, body, jnp.zeros((heads, page), F32))
        if u_sm is not None:
            ol[u_sm] = lse

    def weigh(ls):
        m = functools.reduce(jnp.maximum, ls)
        es = [jnp.exp(l - m) for l in ls]
        total = functools.reduce(jnp.add, es)
        return [e * (1.0 / total) for e in es], m + jnp.log(total)

    def merge(outs, ws, first, count, store):
        def body(i, carry):
            for j in range(MERGE_STEP):
                b = first + i * MERGE_STEP + j
                acc = None
                for o, w in zip(outs, ws):
                    w_b = jnp.sum(jnp.where(lane == b, w, 0.0), axis=1, keepdims=True)
                    t = w_b * o[b].astype(F32)
                    acc = t if acc is None else acc + t
                store(b, acc)
            return carry

        lax.fori_loop(0, count // MERGE_STEP, body, 0)

    n_out = [0]

    def send(src, dst, sem, dev):
        c = remote(src, dst, o_send.at[n_out[0]], sem, dev)
        c.start()
        n_out[0] += 1
        sends.append(c)

    def send_pair(o, l, o_dst, l_dst, sem, dev):
        send(o, o_dst, sem.at[0], dev)
        send(l, l_dst, sem.at[1], dev)

    def arrived(dst, sem):
        remote(dst, dst, o_send.at[0], sem, partner).wait_recv()

    def arrived_pair(o_dst, l_dst, sem):
        arrived(o_dst, sem.at[0])
        arrived(l_dst, sem.at[1])

    def relay(way):
        for i in range(3):
            arrived_pair(ri.at[way, i], rl.at[way, i], r_recv.at[way, i])
        mine = ORDER.index((-1, 's', 0) if way == 0 else (1, 's', 1))
        ws, rfl[way] = weigh([ol[mine]] + [rl[way, i] for i in range(3)])
        outs = [ob.at[mine]] + [ri.at[way, i] for i in range(3)]
        dev = left if way == 0 else right

        def store(b, acc):
            rf[way, b] = acc

        for p in range(PIECES):
            rows = pl.ds(p * piece, piece)
            merge(outs, ws, p * piece, piece, store)
            send(rf.at[way, rows], ff.at[way, rows], f_recv.at[way, p], dev)
            if p == 0:
                send(rfl.at[way], fl.at[way], f_recv.at[way, PIECES], dev)

    for t in range(units + 2):
        if t in before:
            before[t]()
        stage(t)
        if t >= 2:
            u = t - 2
            r, c, half = ORDER[u]
            o, l = ob.at[u], ol.at[u]
            if r == 2:
                dev = (xl if half == 0 else xr) * CORES + c
                send_pair(o, l, ri.at[half, k], rl.at[half, k], r_recv.at[half, k], dev)
            elif r == 0:
                if c == 'o':
                    send_pair(o, l, fp.at[half], fpl.at[half], p_recv.at[half], partner)
            elif (r == -1) == (half == 0):
                if c == 'o':
                    send_pair(o, l, ri.at[half, 2], rl.at[half, 2], r_recv.at[half, 2], partner)
            else:
                dev = (xl if r == -1 else xr) * CORES + c
                send_pair(o, l, fb.at[half, k], fbl.at[half, k], b_recv.at[half, k], dev)
        if t == RELAY_AFTER:
            relay(0)
            relay(1)

    for half in range(2):
        arrived_pair(fp.at[half], fpl.at[half], p_recv.at[half])
        for i in range(CORES):
            arrived_pair(fb.at[half, i], fbl.at[half, i], b_recv.at[half, i])
        mine = ORDER.index((0, 's', half))
        ws, lol[half] = weigh([ol[mine], fpl[half]] + [fbl[half, i] for i in range(CORES)])
        outs = [ob.at[mine], fp.at[half]] + [fb.at[half, i] for i in range(CORES)]

        def store_local(b, acc):
            lo[half, b] = acc

        merge(outs, ws, 0, unit, store_local)

    for half in range(2):
        arrived(fl.at[half], f_recv.at[half, PIECES])
    both = [weigh([lol[half], fl[half]])[0] for half in range(2)]
    for p in range(PIECES):
        for half in range(2):
            arrived(ff.at[half, pl.ds(p * piece, piece)], f_recv.at[half, p])

            def store(b, acc):
                res[half * unit + b] = acc.astype(BF16)

            merge([lo.at[half], ff.at[half]], both[half], p * piece, piece, store)

    for c in sends:
        c.wait_send()


def solution(mesh):
    group = mesh.shape['dcp']
    chips = group // CORES

    def local_step(q_blk, cache_blk, len_blk):
        batch, per_core, width = q_blk.shape
        page = cache_blk.shape[3]
        latent = width - ROPE_DIM
        heads = per_core * group
        rows = batch // group
        unit = rows // 2
        units = batch // unit
        q_own = jnp.transpose(q_blk, (1, 2, 0))
        cache_own = jnp.transpose(cache_blk[:, 0, 0], (0, 2, 1))
        any_spec = pl.BlockSpec(memory_space=pl.ANY)
        dma = pltpu.SemaphoreType.DMA
        vmem = pltpu.VMEM
        return pl.pallas_call(
            functools.partial(kernel, group),
            out_shape=jax.ShapeDtypeStruct((rows, heads, latent), BF16),
            in_specs=[any_spec, any_spec, pl.BlockSpec(memory_space=pltpu.SMEM)],
            out_specs=pl.BlockSpec(memory_space=pltpu.VMEM),
            scratch_shapes=[
                vmem((per_core, width, batch), BF16),
                vmem((group, batch // chips, per_core * width), BF16),
                vmem((group, batch // chips, per_core * width), BF16),
                vmem((group, batch // chips, per_core * width), BF16),
                vmem((group, batch // chips, per_core * width), BF16),
                vmem((batch, width, page), BF16),
                vmem((pl.cdiv(width, LANES), heads * unit, LANES), F32),
                vmem((2, unit, heads, page), F32),
                vmem((2, unit, heads, page), BF16),
                vmem((2, unit, heads, page), F32),
                vmem((units, unit, heads, latent), BF16),
                vmem((units, heads, page), F32),
                vmem((2, 3, unit, heads, latent), BF16),
                vmem((2, 3, heads, page), F32),
                vmem((2, unit, heads, latent), F32),
                vmem((2, heads, page), F32),
                vmem((2, unit, heads, latent), F32),
                vmem((2, heads, page), F32),
                vmem((2, CORES, unit, heads, latent), BF16),
                vmem((2, CORES, heads, page), F32),
                vmem((2, unit, heads, latent), BF16),
                vmem((2, heads, page), F32),
                vmem((2, unit, heads, latent), F32),
                vmem((2, heads, page), F32),
                dma(()),
                dma((units,)),
                dma((28,)),
                dma((group, chips)),
                dma((32,)),
                dma((2, 3, 2)),
                dma((2, PIECES + 1)),
                dma((2, CORES, 2)),
                dma((2, 2)),
            ],
            compiler_params=pltpu.CompilerParams(collective_id=0, has_side_effects=True,
                                                 vmem_limit_bytes=67043328),
        )(q_own, cache_own, len_blk)

    return jax.shard_map(local_step, mesh=mesh, in_specs=(P('dp', 'dcp', None), P('dp', None, 'dcp', None, None), P('dp')), out_specs=P(('dp', 'dcp'), None, None), check_vma=False)
```

time: 77.4 us -> 72.8 us (0.941)
  Pallas kernels: 73.1 us -> 70.8 us
  local copies, waits for them, and re-layouts: 4.01 us -> 1.87 us
    pallas_call x1, Pallas kernels: 73.1 us -> 70.8 us  [local_step(): pl.pallas_call(functools.partial(kernel, group), out_shape=jax.ShapeDtype...]
    unnamed x2 -> x1, local copies, waits for them, and re-layouts: 4.01 us -> 1.87 us
where the time goes in v3:
time: 72.8 us; the launch traced here: 72.7 us
  Pallas kernels  70.8 us (97%)
  local copies, waits for them, and re-layouts  1.87 us (3%)
    pallas_call x1, Pallas kernels, local_step(): pl.pallas_call(functools.partial(kernel, group), out_shape=jax.ShapeDtype...  70.8 us
    unnamed x1, local copies, waits for them, and re-layouts  1.87 us

profile of v3, /device:TPU:81, one launch (start us, length us, event | category | flops | bytes accessed | tf_op | source)
XLA Modules:
  0.0 72.7 jit_solution(7688506565472011565)
XLA Ops:
  0.0 70.8 %shard_map.37 = bf16[32,16,512]{2,1,0:T(8,128)(2,1)} custom-call(bf16[2,576,256]{2,1,0:T(8,128)(2,1)} %bitcast.5, bf16[256,576,128]{2,1,0:T(8,128)(2,1)} %bitcast.4, s32[256]{0:T(256)} %len_ref.1), custom_call_target="tpu_custom_call" | custom-call | tf_op jit(solution)/shard_map/pallas_call | solution.py:336
  70.8 1.9 %copy.5 = bf16[32,16,512]{2,1,0:T(8,128)(2,1)} copy(bf16[32,16,512]{2,1,0:T(8,128)(2,1)} %shard_map.37) | data formatting | bytes 1048576

commit v4 on v3

--- a/solution.py
+++ b/solution.py
@@ -22,11 +22,12 @@
          (-1, 'o', 0), (-1, 0, 1), (-1, 1, 1), (-1, 's', 0),
          (0, 'o', 0), (0, 'o', 1), (0, 's', 0), (0, 's', 1)]
 RELAY_AFTER = 15
-
-
-def kernel(group, q_ref, cache_ref, len_ref, res,
-           qraw, qb0, qb1, qb2, qb3, cv, q32, sb, wb, ib, ob, ol, ri, rl, rf, rfl, ff, fl, fb, fbl, fp, fpl, lo, lol,
-           q_in, c_in, q_send, q_recv, o_send, r_recv, f_recv, b_recv, p_recv):
+HOLD_UNTIL = 5
+
+
+def kernel(group, q_ref, cache_ref, len_hbm, out_hbm,
+           qraw, qb0, qb1, qb2, qb3, cv, q32, sb, wb, ib, ob, ol, ri, rl, rf, rfl, ff, fl, fb, fbl, fp, fpl, lo, lol, len_ref, res,
+           l_in, q_in, c_in, q_send, q_recv, o_send, r_recv, f_recv, b_recv, p_recv, o_out):
     chips = group // CORES
     batch, width, page = cv.shape
     latent = width - ROPE_DIM
@@ -40,9 +41,9 @@
 
     me = lax.axis_index('dcp')
     x, k = me // CORES, me % CORES
-    xr, xl, xf = (x + 1) % chips, (x + chips - 1) % chips, (x + 2) % chips
+    xr, xl = (x + 1) % chips, (x + chips - 1) % chips
     other = 1 - k
-    right, left, far, partner = xr * CORES + k, xl * CORES + k, xf * CORES + k, x * CORES + other
+    right, left, partner = xr * CORES + k, xl * CORES + k, x * CORES + other
 
     def remote(src, dst, send, recv, dev):
         return pltpu.make_async_remote_copy(src_ref=src, dst_ref=dst, send_sem=send, recv_sem=recv,
@@ -62,6 +63,8 @@
     blocks = [qb0, qb1, qb2, qb3]
     own_q = pltpu.make_async_copy(q_ref, qraw, q_in)
     own_q.start()
+    own_len = pltpu.make_async_copy(len_hbm, len_ref, l_in)
+    own_len.start()
 
     barrier = pltpu.get_barrier_semaphore()
     peers = [partner] + [c * CORES + i for c in (xl, xr) for i in range(CORES)]
@@ -77,36 +80,38 @@
         parts.append(jnp.concatenate([qraw[h, latent:, cols] for h in range(2)], axis=0))
         for c, part in enumerate(parts):
             rows = lax.dot_general(pick, part, (((1,), (1,)), ((), ())), preferred_element_type=F32)
-            blocks[s][me, :, c * LANES:(c + 1) * LANES] = rows.astype(BF16)
+            blocks[s][0, :, c * LANES:(c + 1) * LANES] = rows.astype(BF16)
     pl.semaphore_wait(barrier, len(peers))
 
     sends = []
     ME, RIGHT, FAR, LEFT = 0, 1, 2, 3
 
-    def q_copy(src, y, s, dev, to, n):
-        return remote(blocks[(y + s) % chips].at[src], blocks[(y + s - to) % chips].at[src], q_send.at[n], q_recv.at[src, s], dev)
-
-    def q_start(src, y, s, dev, to):
-        c = q_copy(src, y, s, dev, to, len(sends))
+    def q_copy(y, col, s, dev, to, to_col, n):
+        dst = (y - to) % chips * CORES + to_col
+        return remote(blocks[(y + s) % chips].at[y * CORES + col], blocks[(y + s - to) % chips].at[dst],
+                      q_send.at[n], q_recv.at[dst, s], dev)
+
+    def q_start(y, s, to):
+        dev = {ME: partner, RIGHT: right, LEFT: left}[to]
+        c = q_copy(y, 0, s, dev, to, 1 if to == ME else 0, len(sends))
         c.start()
         sends.append(c)
 
-    def q_wait(src, y, s):
-        q_copy(src, y, s, partner, 0, 0).wait_recv()
+    def q_wait(y, col, s):
+        q_copy(y, col, s, partner, 0, col, 0).wait_recv()
 
     def go(s, to):
-        q_start(me, 0, s, {ME: partner, RIGHT: right, LEFT: left}[to], to)
+        q_start(ME, s, to)
 
     def take(y, s, then=None):
-        src = {RIGHT: right, FAR: far, LEFT: left}[y]
-        q_wait(src, y, s)
+        q_wait(y, 0, s)
         if then is not None:
-            q_start(src, y, s, {RIGHT: right, LEFT: left}[then], then)
-        q_start(src, y, s, partner, 0)
+            q_start(y, s, then)
+        q_start(y, s, ME)
 
     def from_partner(own, from_left, from_right, from_far):
-        for y, c, s in ((ME, x, own), (LEFT, xl, from_left), (RIGHT, xr, from_right), (FAR, xf, from_far)):
-            q_wait(c * CORES + other, y, s)
+        for y, s in ((ME, own), (LEFT, from_left), (RIGHT, from_right), (FAR, from_far)):
+            q_wait(y, 1, s)
 
     go(0, RIGHT)
     go(1, LEFT)
@@ -129,6 +134,9 @@
     take(RIGHT, 2, LEFT)
     from_partner(2, 3, 1, 0)
 
+    own_len.wait()
+    held = []
+
     def slot4():
         take(LEFT, 1, RIGHT)
         take(FAR, 3)
@@ -136,18 +144,21 @@
     def slot5():
         take(LEFT, 2)
         take(RIGHT, 0)
+
+    def next_block():
         from_partner(1, 2, 0, 3)
 
     def slot6():
         take(FAR, 1)
         take(FAR, 2)
+        for start in held:
+            start()
+
+    def last_blocks():
         from_partner(3, 0, 2, 1)
         from_partner(0, 1, 3, 2)
 
-    before = {}
-    slot4()
-    slot5()
-    slot6()
+    before = {2: [slot4], 3: [slot5], 4: [next_block], HOLD_UNTIL: [slot6], 8: [last_blocks]}
 
     lane = lax.broadcasted_iota(jnp.int32, (heads, page), 1)
     position = lane + me * page
@@ -163,12 +174,13 @@
             q_block = blocks[r % chips]
             q_rows = pl.ds(pl.multiple_of(core_of(c) * core_rows + half * unit, unit), unit)
 
-            def fill(d, carry):
+            def fill(e, carry):
+                d = (x + e // CORES) % chips * CORES + (k + e) % CORES
                 for h in range(2):
                     rows = pl.ds(pl.multiple_of((d * 2 + h) * unit, unit), unit)
                     for c in range(latent // LANES):
-                        q32[c, rows, :] = q_block[d, q_rows, pl.ds(h * latent + c * LANES, LANES)].astype(F32)
-                    rope = q_block[d, q_rows, pl.ds(2 * latent, LANES)].astype(F32)
+                        q32[c, rows, :] = q_block[e, q_rows, pl.ds(h * latent + c * LANES, LANES)].astype(F32)
+                    rope = q_block[e, q_rows, pl.ds(2 * latent, LANES)].astype(F32)
                     q32[latent // LANES, rows, :] = jnp.where(of_head[h], rope, 0.0)
                 return carry
 
@@ -245,6 +257,22 @@
         arrived(o_dst, sem.at[0])
         arrived(l_dst, sem.at[1])
 
+    def send_unit(u):
+        r, c, half = ORDER[u]
+        o, l = ob.at[u], ol.at[u]
+        if r == 2:
+            dev = (xl if half == 0 else xr) * CORES + c
+            send_pair(o, l, ri.at[half, k], rl.at[half, k], r_recv.at[half, k], dev)
+        elif r == 0:
+            if c == 'o':
+                send_pair(o, l, fp.at[half], fpl.at[half], p_recv.at[half], partner)
+        elif (r == -1) == (half == 0):
+            if c == 'o':
+                send_pair(o, l, ri.at[half, 2], rl.at[half, 2], r_recv.at[half, 2], partner)
+        else:
+            dev = (xl if r == -1 else xr) * CORES + c
+            send_pair(o, l, fb.at[half, k], fbl.at[half, k], b_recv.at[half, k], dev)
+
     def relay(way):
         for i in range(3):
             arrived_pair(ri.at[way, i], rl.at[way, i], r_recv.at[way, i])
@@ -264,25 +292,16 @@
                 send(rfl.at[way], fl.at[way], f_recv.at[way, PIECES], dev)
 
     for t in range(units + 2):
-        if t in before:
-            before[t]()
+        for event in before.get(t, []):
+            event()
         stage(t)
         if t >= 2:
             u = t - 2
-            r, c, half = ORDER[u]
-            o, l = ob.at[u], ol.at[u]
-            if r == 2:
-                dev = (xl if half == 0 else xr) * CORES + c
-                send_pair(o, l, ri.at[half, k], rl.at[half, k], r_recv.at[half, k], dev)
-            elif r == 0:
-                if c == 'o':
-                    send_pair(o, l, fp.at[half], fpl.at[half], p_recv.at[half], partner)
-            elif (r == -1) == (half == 0):
-                if c == 'o':
-                    send_pair(o, l, ri.at[half, 2], rl.at[half, 2], r_recv.at[half, 2], partner)
+            start = functools.partial(send_unit, u)
+            if t < HOLD_UNTIL:
+                held.append(start)
             else:
-                dev = (xl if r == -1 else xr) * CORES + c
-                send_pair(o, l, fb.at[half, k], fbl.at[half, k], b_recv.at[half, k], dev)
+                start()
         if t == RELAY_AFTER:
             relay(0)
             relay(1)
@@ -302,6 +321,7 @@
 
     for half in range(2):
         arrived(fl.at[half], f_recv.at[half, PIECES])
+    done = []
     both = [weigh([lol[half], fl[half]])[0] for half in range(2)]
     for p in range(PIECES):
         for half in range(2):
@@ -311,9 +331,15 @@
                 res[half * unit + b] = acc.astype(BF16)
 
             merge([lo.at[half], ff.at[half]], both[half], p * piece, piece, store)
+            rows = pl.ds(half * unit + p * piece, piece)
+            c = pltpu.make_async_copy(res.at[rows], out_hbm.at[rows], o_out.at[half, p])
+            c.start()
+            done.append(c)
 
     for c in sends:
         c.wait_send()
+    for c in done:
+        c.wait()
 
 
 def solution(mesh):
@@ -336,8 +362,8 @@
         return pl.pallas_call(
             functools.partial(kernel, group),
             out_shape=jax.ShapeDtypeStruct((rows, heads, latent), BF16),
-            in_specs=[any_spec, any_spec, pl.BlockSpec(memory_space=pltpu.SMEM)],
-            out_specs=pl.BlockSpec(memory_space=pltpu.VMEM),
+            in_specs=[any_spec] * 3,
+            out_specs=any_spec,
             scratch_shapes=[
                 vmem((per_core, width, batch), BF16),
                 vmem((group, batch // chips, per_core * width), BF16),
@@ -363,6 +389,9 @@
                 vmem((2, heads, page), F32),
                 vmem((2, unit, heads, latent), F32),
                 vmem((2, heads, page), F32),
+                pltpu.SMEM((batch,), jnp.int32),
+                vmem((rows, heads, latent), BF16),
+                dma(()),
                 dma(()),
                 dma((units,)),
                 dma((28,)),
@@ -372,6 +401,7 @@
                 dma((2, PIECES + 1)),
                 dma((2, CORES, 2)),
                 dma((2, 2)),
+                dma((2, PIECES)),
             ],
             compiler_params=pltpu.CompilerParams(collective_id=0, has_side_effects=True,
                                                  vmem_limit_bytes=67043328),

time: 72.8 us -> 66.8 us (0.918)
  Pallas kernels: 70.8 us -> 64.8 us
    pallas_call x1, Pallas kernels: 70.8 us -> 64.8 us  [local_step(): pl.pallas_call(functools.partial(kernel, group), out_shape=jax.ShapeDtype...]
where the time goes in v4:
time: 66.8 us; the launch traced here: 66.7 us
  Pallas kernels  64.8 us (97%)
  local copies, waits for them, and re-layouts  1.87 us (3%)
    pallas_call x1, Pallas kernels, local_step(): pl.pallas_call(functools.partial(kernel, group), out_shape=jax.ShapeDtype...  64.8 us
    unnamed x1, local copies, waits for them, and re-layouts  1.87 us

profile of v4, /device:TPU:81, one launch (start us, length us, event | category | flops | bytes accessed | tf_op | source)
XLA Modules:
  0.0 66.7 jit_solution(5089996556157147178)
XLA Ops:
  0.0 64.8 %shard_map.37 = bf16[32,16,512]{2,1,0:T(8,128)(2,1)} custom-call(bf16[2,576,256]{2,1,0:T(8,128)(2,1)} %bitcast.5, bf16[256,576,128]{2,1,0:T(8,128)(2,1)} %bitcast.4, s32[256]{0:T(256)} %len_hbm.1), custom_call_target="tpu_custom_call" | custom-call | tf_op jit(solution)/shard_map/pallas_call | solution.py:362
  64.8 1.9 %copy.5 = bf16[32,16,512]{2,1,0:T(8,128)(2,1)} copy(bf16[32,16,512]{2,1,0:T(8,128)(2,1)} %shard_map.37) | data formatting | bytes 1048576

commit v5 on v4

--- a/solution.py
+++ b/solution.py
@@ -22,12 +22,13 @@
          (-1, 'o', 0), (-1, 0, 1), (-1, 1, 1), (-1, 's', 0),
          (0, 'o', 0), (0, 'o', 1), (0, 's', 0), (0, 's', 1)]
 RELAY_AFTER = 15
-HOLD_UNTIL = 5
+HOLD_UNTIL = 4
+TAIL = 16
 
 
 def kernel(group, q_ref, cache_ref, len_hbm, out_hbm,
            qraw, qb0, qb1, qb2, qb3, cv, q32, sb, wb, ib, ob, ol, ri, rl, rf, rfl, ff, fl, fb, fbl, fp, fpl, lo, lol, len_ref, res,
-           l_in, q_in, c_in, q_send, q_recv, o_send, r_recv, f_recv, b_recv, p_recv, o_out):
+           l_in, q_in, c_in, q_send, q_recv, q_tail, o_send, r_recv, f_recv, b_recv, p_recv, o_out):
     chips = group // CORES
     batch, width, page = cv.shape
     latent = width - ROPE_DIM
@@ -86,16 +87,22 @@
     sends = []
     ME, RIGHT, FAR, LEFT = 0, 1, 2, 3
 
-    def q_copy(y, col, s, dev, to, to_col, n):
+    lead = blk - TAIL
+
+    def q_copy(y, col, s, dev, to, to_col, n, sem=None, rows=slice(None)):
         dst = (y - to) % chips * CORES + to_col
-        return remote(blocks[(y + s) % chips].at[y * CORES + col], blocks[(y + s - to) % chips].at[dst],
-                      q_send.at[n], q_recv.at[dst, s], dev)
+        if isinstance(rows, slice):
+            rows = pl.ds(0, lead if y - to in (FAR, -FAR) and s in (1, 2) else blk)
+        return remote(blocks[(y + s) % chips].at[y * CORES + col, rows], blocks[(y + s - to) % chips].at[dst, rows],
+                      q_send.at[n], q_recv.at[dst, s] if sem is None else sem, dev)
+
+    def q_begin(c):
+        c.start()
+        sends.append(c)
 
     def q_start(y, s, to):
         dev = {ME: partner, RIGHT: right, LEFT: left}[to]
-        c = q_copy(y, 0, s, dev, to, 1 if to == ME else 0, len(sends))
-        c.start()
-        sends.append(c)
+        q_begin(q_copy(y, 0, s, dev, to, 1 if to == ME else 0, len(sends)))
 
     def q_wait(y, col, s):
         q_copy(y, col, s, partner, 0, col, 0).wait_recv()
@@ -103,11 +110,20 @@
     def go(s, to):
         q_start(ME, s, to)
 
-    def take(y, s, then=None):
+    def take(y, s, then=None, tail=None):
         q_wait(y, 0, s)
         if then is not None:
             q_start(y, s, then)
+        if tail is not None:
+            chip = {RIGHT: xr, LEFT: xl}[then]
+            for col, core in ((0, k), (1, other)):
+                q_begin(q_copy(y, 0, s, chip * CORES + core, then, col, len(sends), q_tail.at[col, tail], pl.ds(lead, TAIL)))
         q_start(y, s, ME)
+
+    def tails():
+        for tail, s in ((0, 1), (1, 2)):
+            for col in range(CORES):
+                q_copy(FAR, col, s, partner, 0, col, 0, q_tail.at[col, tail], pl.ds(lead, TAIL)).wait_recv()
 
     def from_partner(own, from_left, from_right, from_far):
         for y, s in ((ME, own), (LEFT, from_left), (RIGHT, from_right), (FAR, from_far)):
@@ -131,14 +147,14 @@
     take(RIGHT, 3, LEFT)
     go(0, LEFT)
     take(FAR, 0)
-    take(RIGHT, 2, LEFT)
+    take(RIGHT, 2, LEFT, 1)
     from_partner(2, 3, 1, 0)
 
     own_len.wait()
     held = []
 
     def slot4():
-        take(LEFT, 1, RIGHT)
+        take(LEFT, 1, RIGHT, 0)
         take(FAR, 3)
 
     def slot5():
@@ -155,13 +171,16 @@
             start()
 
     def last_blocks():
+        tails()
         from_partner(3, 0, 2, 1)
         from_partner(0, 1, 3, 2)
 
-    before = {2: [slot4], 3: [slot5], 4: [next_block], HOLD_UNTIL: [slot6], 8: [last_blocks]}
+    before = {2: [slot4], 3: [slot5], 4: [slot6, next_block], 8: [last_blocks]}
 
     lane = lax.broadcasted_iota(jnp.int32, (heads, page), 1)
     position = lane + me * page
+    lse_rows = heads // 2
+    lse_lane = lax.broadcasted_iota(jnp.int32, (lse_rows, LANES), 1)
     rope_lane = lax.broadcasted_iota(jnp.int32, (unit, LANES), 1)
     of_head = [rope_lane < ROPE_DIM, rope_lane >= ROPE_DIM]
 
@@ -199,7 +218,8 @@
                     m = jnp.max(s, axis=1, keepdims=True)
                     w = jnp.exp(s - m)
                     l = jnp.sum(w, axis=1, keepdims=True)
-                    lse = jnp.where(lane == b, m + jnp.log(l), lse)
+                    lse_b = m + jnp.log(l)
+                    lse = jnp.where(lse_lane == b, lse_b[:lse_rows], jnp.where(lse_lane == b + unit, lse_b[lse_rows:], lse))
                 if u_qk is not None:
                     q_b = jnp.concatenate([q32[c, pl.ds(b, heads, stride=unit), :].astype(BF16)
                                            for c in range(latent // LANES + 1)], axis=1)
@@ -214,7 +234,7 @@
                     ib[u_sm % 2, b] = jnp.broadcast_to(1.0 / l, (heads, page))
             return lse
 
-        lse = lax.fori_loop(0, unit // STEP, body, jnp.zeros((heads, page), F32))
+        lse = lax.fori_loop(0, unit // STEP, body, jnp.zeros((lse_rows, LANES), F32))
         if u_sm is not None:
             ol[u_sm] = lse
 
@@ -225,12 +245,13 @@
         return [e * (1.0 / total) for e in es], m + jnp.log(total)
 
     def merge(outs, ws, first, count, store):
-        def body(i, carry):
+        def body(n, carry):
             for j in range(MERGE_STEP):
-                b = first + i * MERGE_STEP + j
+                b = first + n * MERGE_STEP + j
                 acc = None
                 for o, w in zip(outs, ws):
-                    w_b = jnp.sum(jnp.where(lane == b, w, 0.0), axis=1, keepdims=True)
+                    w_b = jnp.concatenate([jnp.sum(jnp.where(lse_lane == b + i * unit, w, 0.0), axis=1, keepdims=True)
+                                           for i in range(2)], axis=0)
                     t = w_b * o[b].astype(F32)
                     acc = t if acc is None else acc + t
                 store(b, acc)
@@ -376,26 +397,27 @@
                 vmem((2, unit, heads, page), BF16),
                 vmem((2, unit, heads, page), F32),
                 vmem((units, unit, heads, latent), BF16),
-                vmem((units, heads, page), F32),
+                vmem((units, heads // 2, LANES), F32),
                 vmem((2, 3, unit, heads, latent), BF16),
-                vmem((2, 3, heads, page), F32),
+                vmem((2, 3, heads // 2, LANES), F32),
                 vmem((2, unit, heads, latent), F32),
-                vmem((2, heads, page), F32),
+                vmem((2, heads // 2, LANES), F32),
                 vmem((2, unit, heads, latent), F32),
-                vmem((2, heads, page), F32),
+                vmem((2, heads // 2, LANES), F32),
                 vmem((2, CORES, unit, heads, latent), BF16),
-                vmem((2, CORES, heads, page), F32),
+                vmem((2, CORES, heads // 2, LANES), F32),
                 vmem((2, unit, heads, latent), BF16),
-                vmem((2, heads, page), F32),
+                vmem((2, heads // 2, LANES), F32),
                 vmem((2, unit, heads, latent), F32),
-                vmem((2, heads, page), F32),
+                vmem((2, heads // 2, LANES), F32),
                 pltpu.SMEM((batch,), jnp.int32),
                 vmem((rows, heads, latent), BF16),
                 dma(()),
                 dma(()),
                 dma((units,)),
-                dma((28,)),
+                dma((32,)),
                 dma((group, chips)),
+                dma((CORES, 2)),
                 dma((32,)),
                 dma((2, 3, 2)),
                 dma((2, PIECES + 1)),

time: 66.8 us -> 64.2 us (0.961); the launches traced: 66.7 us -> 62.9 us
  Pallas kernels: 64.8 us -> 61 us
    pallas_call x1, Pallas kernels: 64.8 us -> 61 us  [local_step(): pl.pallas_call(functools.partial(kernel, group), out_shape=jax.ShapeDtype...]
where the time goes in v5:
time: 64.2 us; the launch traced here: 62.9 us
  Pallas kernels  61 us (95%)
  local copies, waits for them, and re-layouts  1.87 us (3%)
    pallas_call x1, Pallas kernels, local_step(): pl.pallas_call(functools.partial(kernel, group), out_shape=jax.ShapeDtype...  61 us
    unnamed x1, local copies, waits for them, and re-layouts  1.87 us

profile of v5, /device:TPU:81, one launch (start us, length us, event | category | flops | bytes accessed | tf_op | source)
XLA Modules:
  0.0 62.9 jit_solution(919713287915722719)
XLA Ops:
  0.0 61.0 %shard_map.37 = bf16[32,16,512]{2,1,0:T(8,128)(2,1)} custom-call(bf16[2,576,256]{2,1,0:T(8,128)(2,1)} %bitcast.5, bf16[256,576,128]{2,1,0:T(8,128)(2,1)} %bitcast.4, s32[256]{0:T(256)} %len_hbm.1), custom_call_target="tpu_custom_call" | custom-call | tf_op jit(solution)/shard_map/pallas_call | solution.py:383
  61.0 1.9 %copy.5 = bf16[32,16,512]{2,1,0:T(8,128)(2,1)} copy(bf16[32,16,512]{2,1,0:T(8,128)(2,1)} %shard_map.37) | data formatting | bytes 1048576

commit v6 on v5

--- a/solution.py
+++ b/solution.py
@@ -26,9 +26,9 @@
 TAIL = 16
 
 
-def kernel(group, q_ref, cache_ref, len_hbm, out_hbm,
-           qraw, qb0, qb1, qb2, qb3, cv, q32, sb, wb, ib, ob, ol, ri, rl, rf, rfl, ff, fl, fb, fbl, fp, fpl, lo, lol, len_ref, res,
-           l_in, q_in, c_in, q_send, q_recv, q_tail, o_send, r_recv, f_recv, b_recv, p_recv, o_out):
+def kernel(group, q_ref, cache_ref, len_hbm, res,
+           qraw, qb0, qb1, qb2, qb3, cv, q32, sb, wb, ib, ob, ol, ri, rl, rf, rfl, ff, fl, fb, fbl, fp, fpl, lo, lol, len_ref,
+           l_in, q_in, c_in, q_send, q_recv, q_tail, o_send, r_recv, f_recv, b_recv, p_recv):
     chips = group // CORES
     batch, width, page = cv.shape
     latent = width - ROPE_DIM
@@ -342,7 +342,6 @@
 
     for half in range(2):
         arrived(fl.at[half], f_recv.at[half, PIECES])
-    done = []
     both = [weigh([lol[half], fl[half]])[0] for half in range(2)]
     for p in range(PIECES):
         for half in range(2):
@@ -352,15 +351,8 @@
                 res[half * unit + b] = acc.astype(BF16)
 
             merge([lo.at[half], ff.at[half]], both[half], p * piece, piece, store)
-            rows = pl.ds(half * unit + p * piece, piece)
-            c = pltpu.make_async_copy(res.at[rows], out_hbm.at[rows], o_out.at[half, p])
-            c.start()
-            done.append(c)
-
     for c in sends:
         c.wait_send()
-    for c in done:
-        c.wait()
 
 
 def solution(mesh):
@@ -382,9 +374,9 @@
         vmem = pltpu.VMEM
         return pl.pallas_call(
             functools.partial(kernel, group),
-            out_shape=jax.ShapeDtypeStruct((rows, heads, latent), BF16),
+            out_shape=pltpu.VMEM((rows, heads, latent), BF16),
             in_specs=[any_spec] * 3,
-            out_specs=any_spec,
+            out_specs=pl.BlockSpec(memory_space=pltpu.VMEM),
             scratch_shapes=[
                 vmem((per_core, width, batch), BF16),
                 vmem((group, batch // chips, per_core * width), BF16),
@@ -411,7 +403,6 @@
                 vmem((2, unit, heads, latent), F32),
                 vmem((2, heads // 2, LANES), F32),
                 pltpu.SMEM((batch,), jnp.int32),
-                vmem((rows, heads, latent), BF16),
                 dma(()),
                 dma(()),
                 dma((units,)),
@@ -423,10 +414,9 @@
                 dma((2, PIECES + 1)),
                 dma((2, CORES, 2)),
                 dma((2, 2)),
-                dma((2, PIECES)),
             ],
             compiler_params=pltpu.CompilerParams(collective_id=0, has_side_effects=True,
-                                                 vmem_limit_bytes=67043328),
+                                                 vmem_limit_bytes=60000000),
         )(q_own, cache_own, len_blk)
 
     return jax.shard_map(local_step, mesh=mesh, in_specs=(P('dp', 'dcp', None), P('dp', None, 'dcp', None, None), P('dp')), out_specs=P(('dp', 'dcp'), None, None), check_vma=False)

time: 64.2 us -> 62.5 us (0.974)
  local copies, waits for them, and re-layouts: 1.87 us -> 0.8 us
    unnamed x1, local copies, waits for them, and re-layouts: 1.87 us -> 0.8 us
where the time goes in v6:
time: 62.5 us; the launch traced here: 61.3 us
  Pallas kernels  60.4 us (97%)
  local copies, waits for them, and re-layouts  0.8 us (1%)
    pallas_call x1, Pallas kernels, local_step(): pl.pallas_call(functools.partial(kernel, group), out_shape=pltpu.VMEM((ro...  60.4 us

profile of v6, /device:TPU:81, one launch (start us, length us, event | category | flops | bytes accessed | tf_op | source)
XLA Modules:
  0.0 61.3 jit_solution(17139629108078939196)
XLA Ops:
  0.0 60.4 %shard_map.37 = bf16[32,16,512]{2,1,0:T(8,128)(2,1)S(1)} custom-call(bf16[2,576,256]{2,1,0:T(8,128)(2,1)} %bitcast.5, bf16[256,576,128]{2,1,0:T(8,128)(2,1)} %bitcast.4, s32[256]{0:T(256)} %len_hbm.1), custom_call_target="tpu_custom_call" | custom-call | tf_op jit(solution)/shard_map/pallas_call | solution.py:375
  60.5 0.8 %copy.5 = bf16[32,16,512]{2,1,0:T(8,128)(2,1)} copy(bf16[32,16,512]{2,1,0:T(8,128)(2,1)S(1)} %shard_map.37) | data formatting | bytes 1048576

commit v7 on v6

--- a/solution.py
+++ b/solution.py
@@ -13,7 +13,7 @@
 LANES = 128
 STEP = 8
 MERGE_STEP = 4
-PIECES = 2
+PIECES = 4
 MESH = pl.DeviceIdType.MESH
 F32, BF16 = jnp.float32, jnp.bfloat16
 
@@ -409,7 +409,7 @@
                 dma((32,)),
                 dma((group, chips)),
                 dma((CORES, 2)),
-                dma((32,)),
+                dma((36,)),
                 dma((2, 3, 2)),
                 dma((2, PIECES + 1)),
                 dma((2, CORES, 2)),

time: 62.5 us -> 62.4 us (level)
  no operation moved by 1% of the time
where the time goes in v7:
time: 62.4 us; the launch traced here: 61.1 us
  Pallas kernels  60.3 us (97%)
  local copies, waits for them, and re-layouts  0.8 us (1%)
    pallas_call x1, Pallas kernels, local_step(): pl.pallas_call(functools.partial(kernel, group), out_shape=pltpu.VMEM((ro...  60.3 us

profile of v7, /device:TPU:81, one launch (start us, length us, event | category | flops | bytes accessed | tf_op | source)
XLA Modules:
  0.0 61.1 jit_solution(15799711546489912583)
XLA Ops:
  0.0 60.3 %shard_map.37 = bf16[32,16,512]{2,1,0:T(8,128)(2,1)S(1)} custom-call(bf16[2,576,256]{2,1,0:T(8,128)(2,1)} %bitcast.5, bf16[256,576,128]{2,1,0:T(8,128)(2,1)} %bitcast.4, s32[256]{0:T(256)} %len_hbm.1), custom_call_target="tpu_custom_call" | custom-call | tf_op jit(solution)/shard_map/pallas_call | solution.py:375
  60.3 0.8 %copy.5 = bf16[32,16,512]{2,1,0:T(8,128)(2,1)} copy(bf16[32,16,512]{2,1,0:T(8,128)(2,1)S(1)} %shard_map.37) | data formatting | bytes 1048576
